TPU v7x, 32 devices: a whole 2x2x4 slice. The times are simulated.
32 devices in a mesh: rep: 4 (over x, core), shard: 8 (over z, y).
Axes of the slice: x: 2, y: 2, z: 4, core: 2. Of those that a mesh axis runs over, the one named last changes fastest.
Arguments:
- images: bfloat16 [32, 256, 1152], P(('rep', 'shard')), may hold values from -6 to 6
- cotangent: bfloat16 [32, 256, 1152], P(('rep', 'shard')), may hold values from -6 to 6
- w_qkv: bfloat16 [1152, 3456], P('shard'), may hold values from -2 to 2
- w_out: bfloat16 [1152, 1152], P('shard'), may hold values from -0.75 to 0.75
- w_up: bfloat16 [1152, 4304], P('shard'), may hold values from -0.1875 to 0.1875
- w_down: bfloat16 [1152, 4304], P('shard'), may hold values from -0.125 to 0.125
- vectors: bfloat16 [1152, 8], P('shard'), may hold values from -3 to 3, as said below
- up_bias: bfloat16 [4304], replicated, may hold values from -3 to 3
Outputs:
- outputs: bfloat16 [32, 256, 1152], P(('rep', 'shard'))
- input_grad: bfloat16 [32, 256, 1152], P(('rep', 'shard'))
- qkv_grad: float32 [1152, 3456], P('shard')
- out_grad: float32 [1152, 1152], P('shard')
- up_grad: float32 [1152, 4304], P('shard')
- down_grad: float32 [1152, 4304], P('shard')
- vectors_grad: float32 [1152, 8], P('shard')
- up_bias_grad: float32 [4304], replicated
Inputs may be any that keep to these rules, and one draw needn't show every extreme that they name: `vectors`: columns 0 and 5 (the norms' gains) are positive; the other columns have either sign.
All inputs are finite; a program needn't handle non-finite values.
Results may differ from a plain program's by a relative error of at most 0.014.
Values may be sent and summed in bfloat16 or wider, within the bound.
A program may use at most 256 MiB of HBM per device.

v0:
```python
import math
import jax
import jax.numpy as jnp
from jax import lax
from jax.sharding import PartitionSpec as P

HEAD_DIM = 72
EPSILON = 1e-06
GELU_COEF = 0.044715
ROOT_TWO_PI = math.sqrt(2.0 / math.pi)
F32 = jnp.float32
BF16 = jnp.bfloat16


def dot(a, b, ca, cb):
    return lax.dot_general(a, b, (((ca,), (cb,)), ((), ())), preferred_element_type=F32)


def batched(pattern, left_op, right_op):
    return jnp.einsum(pattern, left_op, right_op, preferred_element_type=F32)


def norm_rows(hidden):
    row_mean = jnp.mean(hidden, axis=-1, keepdims=True)
    centered = hidden - row_mean
    variance = jnp.mean(centered * centered, axis=-1, keepdims=True)
    inv_std = lax.rsqrt(variance + EPSILON)
    return (centered * inv_std, inv_std)


def norm_back(grad_normed, normed, inv_std):
    mean_grad = jnp.mean(grad_normed, axis=-1, keepdims=True)
    mean_proj = jnp.mean(grad_normed * normed, axis=-1, keepdims=True)
    return inv_std * (grad_normed - mean_grad - normed * mean_proj)


def gelu_parts(u):
    t = jnp.tanh(ROOT_TWO_PI * (u + GELU_COEF * u * u * u))
    act = 0.5 * u * (1.0 + t)
    der = 0.5 * (1.0 + t) + 0.5 * u * (1.0 - t * t) * ROOT_TWO_PI * (1.0 + 3.0 * GELU_COEF * u * u)
    return (act, der)


def gather_rep(a):
    return lax.all_gather(a, "rep", axis=0, tiled=True)


def scatter_rep(a):
    return lax.psum_scatter(a.astype(BF16), "rep", scatter_dimension=0, tiled=True).astype(F32)


def per_device(reps, images, cotangent, w_qkv, w_out, w_up, w_down, vectors, up_bias):
    r = lax.axis_index("rep")
    batch, seq, width = images.shape
    rows = w_qkv.shape[0]
    quarter = width // reps
    ffq = w_up.shape[1] // reps
    heads = quarter // HEAD_DIM

    def take(w, start, size):
        return lax.dynamic_slice_in_dim(w, start, size, 1)

    part = jnp.concatenate(
        [take(w_qkv, t * width + r * quarter, quarter) for t in range(3)], axis=1
    )
    mine_up = take(w_up, r * ffq, ffq)
    mine_down = take(w_down, r * ffq, ffq)
    wq = lax.all_gather(part, "shard", axis=0, tiled=True)
    wo = lax.all_gather(w_out, "shard", axis=0, tiled=True)
    wu = lax.all_gather(mine_up, "shard", axis=0, tiled=True)
    wd = lax.all_gather(mine_down, "shard", axis=0, tiled=True)
    params = lax.all_gather(vectors, "shard", axis=0, tiled=True).astype(F32)
    wo = lax.dynamic_slice_in_dim(wo, r * quarter, quarter, 0)
    bias_up = lax.dynamic_slice_in_dim(up_bias, r * ffq, ffq, 0).astype(F32)
    x = images.reshape(batch * seq, width).astype(F32)
    e = cotangent.reshape(batch * seq, width)
    e_all = gather_rep(e)
    n1, r1 = norm_rows(x)
    a1 = gather_rep((n1 * params[:, 0] + params[:, 1]).astype(BF16))
    proj = dot(a1, wq, 1, 0)
    bq = lax.dynamic_slice_in_dim(params[:, 2], r * quarter, quarter, 0)
    bv = lax.dynamic_slice_in_dim(params[:, 3], r * quarter, quarter, 0)
    group = reps * batch

    def split(t):
        return t.reshape(group, seq, heads, HEAD_DIM)

    q = split((proj[:, :quarter] + bq).astype(BF16))
    k = split(proj[:, quarter : 2 * quarter].astype(BF16))
    v = split((proj[:, 2 * quarter :] + bv).astype(BF16))
    scale = 1.0 / math.sqrt(HEAD_DIM)
    s = batched("bqhd,bkhd->bhqk", q, k) * scale
    top = jnp.max(s, axis=-1, keepdims=True)
    ex = jnp.exp(s - top)
    total = jnp.sum(ex, axis=-1, keepdims=True)
    probs = ex / total
    probs_bf = probs.astype(BF16)
    o = batched("bhqk,bkhd->bqhd", probs_bf, v).reshape(group * seq, quarter).astype(BF16)
    m = x + scatter_rep(dot(o, wo, 1, 0)) + params[:, 4]
    n2, r2 = norm_rows(m)
    a2 = gather_rep((n2 * params[:, 5] + params[:, 6]).astype(BF16))
    act, der = gelu_parts(dot(a2, wu, 1, 0) + bias_up)
    act = act.astype(BF16)
    final = m + scatter_rep(dot(act, wd, 1, 1)) + params[:, 7]
    outputs = final.astype(BF16).reshape(batch, seq, width)

    def reduce_rows(term):
        return lax.psum_scatter(term.astype(BF16), "shard", scatter_dimension=0, tiled=True)

    ef = e.astype(F32)
    g_down = reduce_rows(dot(e_all, act, 0, 0))
    du = dot(e_all, wd, 1, 0) * der
    upb = jnp.sum(du, axis=0)
    dub = du.astype(BF16)
    g_up = reduce_rows(dot(a2, dub, 0, 0))
    da2 = scatter_rep(dot(dub, wu, 1, 1))
    dm = ef + norm_back(da2 * params[:, 5], n2, r2)
    dmb = gather_rep(dm.astype(BF16))
    do = dot(dmb, wo, 1, 1).astype(BF16)
    out_term = dot(o, dmb, 0, 0).astype(BF16)
    out_term = lax.dynamic_update_slice_in_dim(
        jnp.zeros((width, width), BF16), out_term, r * quarter, 0
    )
    g_out = lax.psum_scatter(out_term, "shard", scatter_dimension=0, tiled=True)
    do = split(do)
    dv = batched("bhqk,bqhd->bkhd", probs_bf, do)
    dpr = batched("bqhd,bkhd->bhqk", do, v)
    delta = jnp.sum(probs * dpr, axis=-1, keepdims=True)
    ds = (probs * (dpr - delta) * scale).astype(BF16)
    dq = batched("bhqk,bkhd->bqhd", ds, k)
    dk = batched("bhqk,bqhd->bkhd", ds, q)
    dp = jnp.concatenate([t.reshape(group * seq, quarter) for t in (dq, dk, dv)], axis=1)
    col = jnp.sum(dp, axis=0)
    dp = dp.astype(BF16)
    g_qkv = reduce_rows(dot(a1, dp, 0, 0))
    da1 = scatter_rep(dot(dp, wq, 1, 1))
    input_grad = dm + norm_back(da1 * params[:, 0], n1, r1)
    input_grad = input_grad.astype(BF16).reshape(batch, seq, width)

    def place(piece):
        return lax.dynamic_update_slice_in_dim(jnp.zeros((width,), F32), piece, r * quarter, 0)

    vec = jnp.stack(
        [
            jnp.sum(da1 * n1, axis=0),
            jnp.sum(da1, axis=0),
            place(col[:quarter]),
            place(col[2 * quarter :]),
            jnp.sum(dm, axis=0),
            jnp.sum(da2 * n2, axis=0),
            jnp.sum(da2, axis=0),
            jnp.sum(ef, axis=0),
        ],
        axis=1,
    )
    vec = lax.psum(lax.psum_scatter(vec, "shard", scatter_dimension=0, tiled=True), "rep")
    upb = lax.all_gather(lax.psum(upb, "shard"), "rep", axis=0, tiled=True)

    def columns(g):
        return lax.all_gather(g, "rep", axis=0).transpose(1, 0, 2).astype(F32)

    g_down = columns(g_down).reshape(rows, -1)
    g_up = columns(g_up).reshape(rows, -1)
    g_qkv = columns(g_qkv).reshape(rows, reps, 3, quarter).transpose(0, 2, 1, 3).reshape(rows, -1)
    g_out = lax.psum(g_out, "rep").astype(F32)
    return (outputs, input_grad, g_qkv, g_out, g_up, g_down, vec, upb)


def solution(mesh):
    reps = mesh.shape["rep"]
    token = P(("rep", "shard"), None, None)
    row = P("shard", None)

    def body(*args):
        return per_device(reps, *args)

    return jax.shard_map(
        body,
        mesh=mesh,
        in_specs=(token, token, row, row, row, row, row, P()),
        out_specs=(token, token, row, row, row, row, row, P()),
        check_vma=False,
    )
```

profile of v0, /device:TPU:0, one launch (start us, length us, event | category | flops | bytes accessed | tf_op | source)
XLA Modules:
  0.0 929.8 jit_solution(6168868636376953412)
XLA Ops:
  9.5 32.7 %all-gather.4 = bf16[8,144,8]{1,2,0:T(8,128)(2,1)S(1)} all-gather(bf16[1,144,8]{1,2,0:T(8,128)(2,1)} %bitcast.161), channel_id=1, replica_groups=mesh['rep'=4,'shard'=8] {'shard'}, dimensions={0}, use_global_device_ids=true | all-gather | bytes 20736 | tf_op jit(solution)/shard_map/all_gather | solution.py:72
  46.0 16.3 %all-gather.18.cloned.1.call-done = bf16[1152,864]{1,0:T(8,128)(2,1)} async-done(((bf16[144,864]{1,0:T(8,128)(2,1)}), bf16[1152,864]{1,0:T(8,128)(2,1)}) %all-gather.18.cloned.1.call-update) | async-done | bytes 1990672 | tf_op jit(solution)/shard_map/all_gather | solution.py:68
  62.3 24.8 %all-gather.16.cloned.1.call-done = bf16[1024,1152]{1,0:T(8,128)(2,1)} async-done(((bf16[256,1152]{1,0:T(8,128)(2,1)}), bf16[1024,1152]{1,0:T(8,128)(2,1)}) %all-gather.16.cloned.1.call-update) | async-done | bytes 2359312 | tf_op jit(solution)/shard_map/all_gather | solution.py:45
  104.5 39.8 %all-gather.20.cloned.1.call-done = bf16[1152,1152]{1,0:T(8,128)(2,1)} async-done(((bf16[144,1152]{1,0:T(8,128)(2,1)}), bf16[1152,1152]{1,0:T(8,128)(2,1)}) %all-gather.20.cloned.1.call-update) | async-done | bytes 2654224 | tf_op jit(solution)/shard_map/all_gather | solution.py:69
  149.4 30.5 %reduce-scatter.14.cloned.1.call-done = bf16[256,1152]{1,0:T(8,128)(2,1)} async-done(((bf16[1024,1152]{1,0:T(8,128)(2,1)}), bf16[256,1152]{1,0:T(8,128)(2,1)}) %reduce-scatter.14.cloned.1.call-update) | async-done | bytes 589840 | tf_op jit(solution)/shard_map/reduce_scatter | solution.py:49
  187.7 49.8 %all-gather.24.cloned.1.call-done = bf16[1152,1076]{1,0:T(8,128)(2,1)} async-done(((bf16[144,1076]{1,0:T(8,128)(2,1)}), bf16[1152,1076]{1,0:T(8,128)(2,1)}) %all-gather.24.cloned.1.call-update) | async-done | bytes 2479120 | tf_op jit(solution)/shard_map/all_gather | solution.py:70
  237.5 24.6 %all-gather.22.cloned.1.call-done = bf16[1024,1152]{1,0:T(8,128)(2,1)} async-done(((bf16[256,1152]{1,0:T(8,128)(2,1)}), bf16[1024,1152]{1,0:T(8,128)(2,1)}) %all-gather.22.cloned.1.call-update) | async-done | bytes 2359312 | tf_op jit(solution)/shard_map/all_gather | solution.py:45
  262.1 7.5 convolution_add_fusion
  269.7 18.1 %all-gather.30.cloned.1.call-done = bf16[1,1024,1152]{2,1,0:T(8,128)(2,1)} async-done(((bf16[1,256,1152]{2,1,0:T(8,128)(2,1)}), bf16[1,1024,1152]{2,1,0:T(8,128)(2,1)}) %all-gather.30.cloned.1.call-update) | async-done | bytes 2359312 | tf_op jit(solution)/shard_map/all_gather | solution.py:45
  287.7 57.8 %all-gather.26.cloned.1.call-done = bf16[1152,1076]{1,0:T(8,128)(2,1)} async-done(((bf16[144,1076]{1,0:T(8,128)(2,1)}), bf16[1152,1076]{1,0:T(8,128)(2,1)}) %all-gather.26.cloned.1.call-update) | async-done | bytes 2479120 | tf_op jit(solution)/shard_map/all_gather | solution.py:71
  345.5 8.8 fusion.98
  361.1 8.8 convolution_convert_fusion.5
  370.0 7.2 convolution_convert_fusion.1
  377.3 8.3 fusion.2
  385.7 5.2 copy.96
  394.0 33.4 %reduce-scatter.16.cloned.1.call-done = bf16[256,1152]{1,0:T(8,128)(2,1)} async-done(((bf16[1024,1152]{1,0:T(8,128)(2,1)}), bf16[256,1152]{1,0:T(8,128)(2,1)}) %reduce-scatter.16.cloned.1.call-update) | async-done | bytes 589840 | tf_op jit(solution)/shard_map/reduce_scatter | solution.py:49
  431.2 71.1 %reduce-scatter.26.cloned.1.call-done = bf16[144,1076]{1,0:T(8,128)(2,1)} async-done(((bf16[1152,1076]{1,0:T(8,128)(2,1)}), bf16[144,1076]{1,0:T(8,128)(2,1)}) %reduce-scatter.26.cloned.1.call-update) | async-done | bytes 309904 | tf_op jit(solution)/shard_map/reduce_scatter | solution.py:108
  502.4 74.0 %reduce-scatter.28.cloned.1.call-done = bf16[144,1076]{1,0:T(8,128)(2,1)} async-done(((bf16[1152,1076]{1,0:T(8,128)(2,1)}), bf16[144,1076]{1,0:T(8,128)(2,1)}) %reduce-scatter.28.cloned.1.call-update) | async-done | bytes 309904 | tf_op jit(solution)/shard_map/reduce_scatter | solution.py:108
  576.6 25.0 %all-gather.28.cloned.1.call-done = bf16[1024,1152]{1,0:T(8,128)(2,1)} async-done(((bf16[256,1152]{1,0:T(8,128)(2,1)}), bf16[1024,1152]{1,0:T(8,128)(2,1)}) %all-gather.28.cloned.1.call-update) | async-done | bytes 2359312 | tf_op jit(solution)/shard_map/all_gather | solution.py:45
  614.9 8.4 fusion.42
  626.6 8.7 fusion.39
  645.2 7.0 convolution_convert_fusion.2
  658.7 21.7 %psum.23 = f32[1076]{0:T(1024)S(1)} all-reduce(f32[1076]{0:T(1024)S(1)} %get-tuple-element.44), channel_id=1, replica_groups=mesh['rep'=4,'shard'=8] {'shard'}, use_global_device_ids=true, to_apply=%region_30.0 | all-reduce | flops 1076 | bytes 8608 | tf_op jit(solution)/shard_map/psum | solution.py:157
  699.8 12.9 %reduce-scatter.22.cloned.1.call-done = bf16[144,864]{1,0:T(8,128)(2,1)} async-done(((bf16[1152,864]{1,0:T(8,128)(2,1)}), bf16[144,864]{1,0:T(8,128)(2,1)}) %reduce-scatter.22.cloned.1.call-update) | async-done | bytes 248848 | tf_op jit(solution)/shard_map/reduce_scatter | solution.py:108
  712.7 10.4 %all-gather.1 = bf16[576,864]{1,0:T(8,128)(2,1)S(1)} all-gather(bf16[144,864]{1,0:T(8,128)(2,1)} %reduce-scatter.22.cloned.1.call-done), channel_id=3, replica_groups=mesh['rep'=4,'shard'=8] {'rep'}, dimensions={0}, use_global_device_ids=true | all-gather | bytes 1244160 | tf_op jit(solution)/shard_map/all_gather | solution.py:160
  724.5 5.2 reshape.159
  729.8 5.7 copy.88
  739.0 7.9 reduce-scatter.20.cloned.1.call-done
  749.8 72.2 %reduce-scatter.24.cloned.1.call-done = bf16[144,1152]{1,0:T(8,128)(2,1)} async-done(((bf16[1152,1152]{1,0:T(8,128)(2,1)}), bf16[144,1152]{1,0:T(8,128)(2,1)}) %reduce-scatter.24.cloned.1.call-update) | async-done | bytes 331792 | tf_op jit(solution)/shard_map/reduce_scatter | solution.py:124
  824.5 63.2 %reduce-scatter.30.cloned.1.call-done = f32[144,8]{1,0:T(8,128)} async-done(((f32[1152,8]{1,0:T(8,128)}), f32[144,8]{1,0:T(8,128)}) %reduce-scatter.30.cloned.1.call-update) | async-done | bytes 4624
  888.6 10.9 %all-reduce.1 = (f32[144,8]{0,1:T(8,128)}, f32[4304]{0:T(1024)}) all-reduce(f32[144,8]{0,1:T(8,128)S(1)} %copy.99, f32[4304]{0:T(1024)S(1)} %dynamic-update-slice), channel_id=1, replica_groups=mesh['rep'=4,'shard'=8] {'rep'}, use_global_device_ids=true, to_apply=%region_28.0 | all-reduce | flops 5456 | bytes 43648 | tf_op jit(solution)/shard_map/psum | solution.py:156
  899.5 21.2 %all-reduce.4.cloned.1.call-done = bf16[144,1152]{1,0:T(8,128)(2,1)} async-done(((bf16[144,1152]{1,0:T(8,128)(2,1)}), bf16[144,1152]{1,0:T(8,128)(2,1)}) %all-reduce.4.cloned.1.call-update) | async-done | bytes 331792 | tf_op jit(solution)/shard_map/psum | solution.py:165
  (176 shorter events, 114.7 us)
Async XLA Ops:
  7.2 141.2 %copy-start = (bf16[144,4304]{1,0:T(8,128)(2,1)S(1)}, bf16[144,4304]{1,0:T(8,128)(2,1)}, u32[]{:S(2)}) copy-start(bf16[144,4304]{1,0:T(8,128)(2,1)} %param.12) | copy-start | bytes 3718660
  7.2 36.4 %copy-start.2 = (bf16[1,256,1152]{2,1,0:T(8,128)(2,1)S(1)}, bf16[1,256,1152]{2,1,0:T(8,128)(2,1)}, u32[]{:S(2)}) copy-start(bf16[1,256,1152]{2,1,0:T(8,128)(2,1)} %param.8) | copy-start | bytes 1769476
  7.2 55.1 %all-gather.18.cloned.1.call-start = ((), (), s32[]{:S(2)}) async-start(), calls=%async_computation.10 | async-start | bytes 2322432 | tf_op jit(solution)/shard_map/all_gather | solution.py:68
  9.5 77.6 %all-gather.16.cloned.1.call-start = ((), (), s32[]{:S(2)}) async-start(), calls=%async_computation.9 | async-start | bytes 2949120 | tf_op jit(solution)/shard_map/all_gather | solution.py:45
  45.1 99.2 %all-gather.20.cloned.1.call-start = ((), (), s32[]{:S(2)}) async-start(), calls=%async_computation.11 | async-start | bytes 2985984 | tf_op jit(solution)/shard_map/all_gather | solution.py:69
  45.8 134.0 %reduce-scatter.14.cloned.1.call-start = ((), (), s32[]{:S(2)}) async-start(), calls=%async_computation.12 | async-start | bytes 2949120 | tf_op jit(solution)/shard_map/reduce_scatter | solution.py:49
  94.7 4.0 copy-start.9
  96.7 5.3 copy-start.12
  104.5 43.8 %copy-start.16 = (bf16[36,8,4,256]{3,1,2,0:T(8,128)(2,1)}, bf16[36,8,4,256]{3,1,2,0:T(8,128)(2,1)S(1)}, u32[]{:S(2)}) copy-start(bf16[36,8,4,256]{3,1,2,0:T(8,128)(2,1)S(1)} %copy.100) | copy-start | bytes 1769476
  148.3 89.1 %all-gather.24.cloned.1.call-start = ((), (), s32[]{:S(2)}) async-start(), calls=%async_computation.14 | async-start | bytes 2985984 | tf_op jit(solution)/shard_map/all_gather | solution.py:70
  149.3 112.8 %all-gather.22.cloned.1.call-start = ((), (), s32[]{:S(2)}) async-start(), calls=%async_computation.13 | async-start | bytes 2949120 | tf_op jit(solution)/shard_map/all_gather | solution.py:45
  179.9 2.9 copy-start.3
  183.9 103.8 %all-gather.30.cloned.1.call-start = ((), (), s32[]{:S(2)}) async-start(), calls=%async_computation.24 | async-start | bytes 2949120 | tf_op jit(solution)/shard_map/all_gather | solution.py:45
  184.7 160.8 %all-gather.26.cloned.1.call-start = ((), (), s32[]{:S(2)}) async-start(), calls=%async_computation.15 | async-start | bytes 2985984 | tf_op jit(solution)/shard_map/all_gather | solution.py:71
  186.7 205.5 %reduce-scatter.18.cloned.1.call-start = ((), (), s32[]{:S(2)}) async-start(), calls=%async_computation.17 | async-start | bytes 2949120 | tf_op jit(solution)/shard_map/reduce_scatter | solution.py:49
  345.5 10.2 %copy-start.18 = (bf16[1152,1076]{1,0:T(8,128)(2,1)S(1)}, bf16[1152,1076]{1,0:T(8,128)(2,1)}, u32[]{:S(2)}) copy-start(bf16[1152,1076]{1,0:T(8,128)(2,1)} %all-gather.24.cloned.1.call-done) | copy-start | bytes 7437316
  360.7 66.7 %reduce-scatter.16.cloned.1.call-start = ((), (), s32[]{:S(2)}) async-start(), calls=%async_computation.16 | async-start | bytes 2949120 | tf_op jit(solution)/shard_map/reduce_scatter | solution.py:49
  370.0 132.3 %reduce-scatter.26.cloned.1.call-start = ((), (), s32[]{:S(2)}) async-start(), calls=%async_computation.23 | async-start | bytes 2985984 | tf_op jit(solution)/shard_map/reduce_scatter | solution.py:108
  377.3 199.1 %reduce-scatter.28.cloned.1.call-start = ((), (), s32[]{:S(2)}) async-start(), calls=%async_computation.27 | async-start | bytes 2985984 | tf_op jit(solution)/shard_map/reduce_scatter | solution.py:108
  390.9 36.5 %copy-start.5 = (bf16[1,256,1152]{2,1,0:T(8,128)(2,1)S(1)}, bf16[1,256,1152]{2,1,0:T(8,128)(2,1)}, u32[]{:S(2)}) copy-start(bf16[1,256,1152]{2,1,0:T(8,128)(2,1)} %param.9) | copy-start | bytes 1769476
  390.9 210.6 %all-gather.28.cloned.1.call-start = ((), (), s32[]{:S(2)}) async-start(), calls=%async_computation.18 | async-start | bytes 2949120 | tf_op jit(solution)/shard_map/all_gather | solution.py:45
  431.2 249.7 %all-gather.32.cloned.1.call-start = ((), (), s32[]{:S(2)}) async-start(), calls=%async_computation.25 | async-start | bytes 1658880 | tf_op jit(solution)/shard_map/all_gather | solution.py:160
  502.3 186.5 %all-gather.34.cloned.1.call-start = ((), (), s32[]{:S(2)}) async-start(), calls=%async_computation.26 | async-start | bytes 1658880 | tf_op jit(solution)/shard_map/all_gather | solution.py:160
  576.4 136.3 %reduce-scatter.22.cloned.1.call-start = ((), (), s32[]{:S(2)}) async-start(), calls=%async_computation.20 | async-start | bytes 2322432 | tf_op jit(solution)/shard_map/reduce_scatter | solution.py:108
  606.9 3.2 copy-start.14
  623.2 3.3 copy-start.10
  644.9 102.0 %reduce-scatter.20.cloned.1.call-start = ((), (), s32[]{:S(2)}) async-start(), calls=%async_computation.19 | async-start | bytes 2949120 | tf_op jit(solution)/shard_map/reduce_scatter | solution.py:49
  652.2 169.8 %reduce-scatter.24.cloned.1.call-start = ((), (), s32[]{:S(2)}) async-start(), calls=%async_computation.21 | async-start | bytes 2985984 | tf_op jit(solution)/shard_map/reduce_scatter | solution.py:124
  652.3 2.8 copy-start.20
  656.9 230.8 %reduce-scatter.30.cloned.1.call-start = ((), (), s32[]{:S(2)}) async-start(), calls=%async_computation.28 | async-start | bytes 663552
  749.7 172.8 %copy-start.1 = (bf16[144,4304]{1,0:T(8,128)(2,1)S(1)}, bf16[144,4304]{1,0:T(8,128)(2,1)}, u32[]{:S(2)}) copy-start(bf16[144,4304]{1,0:T(8,128)(2,1)} %param.12) | copy-start | bytes 3718660
  749.8 170.9 %all-reduce.4.cloned.1.call-start = ((), (), s32[]{:S(2)}) async-start(), calls=%async_computation.22 | async-start | bytes 663552 | tf_op jit(solution)/shard_map/psum | solution.py:165
  (11 other events, 18.5 us)
Sparse Core Ops, SparseCore 0:
  10.8 51.4 all-gather.17
  64.4 22.6 all-gather.15
  89.3 54.9 all-gather.19
  148.4 31.3 reduce-scatter.13
  182.5 54.9 all-gather.23
  239.5 22.6 all-gather.21
  263.7 24.0 all-gather.29
  290.5 54.9 all-gather.25
  360.8 31.3 reduce-scatter.17
  394.6 32.8 reduce-scatter.15
  431.1 71.1 reduce-scatter.25
  505.8 70.4 reduce-scatter.27
  578.5 23.0 all-gather.27
  603.0 18.2 all-gather.31
  622.7 18.2 all-gather.33
  645.0 67.6 reduce-scatter.21
  715.1 31.7 reduce-scatter.19
  750.4 71.6 reduce-scatter.23
  825.9 61.6 reduce-scatter.29
  889.9 30.7 all-reduce.3
where the time goes:
time: 939 us; the launch traced here: 930 us
  waiting for transfers between devices  645 us (69%)
  matrix products  96.5 us (10%)
  blocking collectives  75.6 us (8%)
  local copies, waits for them, and re-layouts  63.5 us (7%)
  other arithmetic  30.9 us (3%)
  between operations  15.9 us (2%)
    reduce_scatter x3, waiting for transfers between devices, reduce_rows(): lax.psum_scatter(term.astype(BF16), 'shard', scatter_dimension=0, tiled=T...  158 us
    all_gather x4, waiting for transfers between devices, gather_rep(): return lax.all_gather(a, 'rep', axis=0, tiled=True)  92.5 us
    reduce_scatter x4, waiting for transfers between devices, scatter_rep(): lax.psum_scatter(a.astype(BF16), 'rep', scatter_dimension=0, tiled=True)  73.1 us
    reduce_scatter x1, waiting for transfers between devices, per_device(): g_out = lax.psum_scatter(out_term, 'shard', scatter_dimension=0, tiled=True)  72.2 us
    dot_general x12, matrix products, dot(): lax.dot_general(a, b, (((ca,), (cb,)), ((), ())), preferred_element_type=...  71 us
    unnamed x21, waiting for transfers between devices  64.9 us
    all_gather x1, waiting for transfers between devices, per_device(): wd = lax.all_gather(mine_down, 'shard', axis=0, tiled=True)  57.8 us
    all_gather x1, waiting for transfers between devices, per_device(): wu = lax.all_gather(mine_up, 'shard', axis=0, tiled=True)  49.8 us
  transfers between devices with their start and end apart: 20, of which 18 were waited for; matrix products, arithmetic and copies ran while one was open for 17% of the time, Pallas kernels for 0%

commit v1 on v0

--- a/solution.py
+++ b/solution.py
@@ -10,6 +10,19 @@
 ROOT_TWO_PI = math.sqrt(2.0 / math.pi)
 F32 = jnp.float32
 BF16 = jnp.bfloat16
+
+
+def ring_gather(shard, axis, dim):
+    ways = lax.axis_size(axis)
+    up = [(d, (d + 1) % ways) for d in range(ways)]
+    down = [(d, (d - 1) % ways) for d in range(ways)]
+    earlier, later = ([shard], [shard])
+    for _ in range(ways // 2):
+        earlier.append(lax.ppermute(earlier[-1], axis, up))
+    for _ in range((ways - 1) // 2):
+        later.append(lax.ppermute(later[-1], axis, down))
+    line = jnp.concatenate([*earlier[::-1], *later[1:]], axis=dim)
+    return jnp.roll(line, (lax.axis_index(axis) - ways // 2) * shard.shape[dim], axis=dim)
 
 
 def dot(a, b, ca, cb):
@@ -42,7 +55,7 @@
 
 
 def gather_rep(a):
-    return lax.all_gather(a, "rep", axis=0, tiled=True)
+    return ring_gather(a, "rep", 0)
 
 
 def scatter_rep(a):

time: 939 us -> 846 us (0.901)
  waiting for transfers between devices: 645 us -> 514 us
  other arithmetic: 30.9 us -> 70.8 us
    all_gather x4 -> x0, waiting for transfers between devices: 92.5 us -> none  [gather_rep(): return lax.all_gather(a, 'rep', axis=0, tiled=True)]
    ppermute x0 -> x12, waiting for transfers between devices: none -> 58 us  [the longest x8 56.9 us: ring_gather(): earlier.append(lax.ppermute(earlier[-1], axis, up))]
    all_gather x1, waiting for transfers between devices: 49.8 us -> 3.71 us  [per_device(): wu = lax.all_gather(mine_up, 'shard', axis=0, tiled=True)]
    concatenate x0 -> x4, other arithmetic: none -> 42.5 us  [ring_gather(): jnp.roll(line, (lax.axis_index(axis) - ways // 2) * shard.shape[dim], axi...]
    all_gather x1, waiting for transfers between devices: 39.8 us -> 22.1 us  [per_device(): wo = lax.all_gather(w_out, 'shard', axis=0, tiled=True)]
    all_gather x1, waiting for transfers between devices: 16.3 us -> 0.01 us  [per_device(): wq = lax.all_gather(part, 'shard', axis=0, tiled=True)]
    reduce_scatter x3, waiting for transfers between devices: 158 us -> 146 us  [reduce_rows(): lax.psum_scatter(term.astype(BF16), 'shard', scatter_dimension=0, tiled=T...]
    unnamed x21 -> x17, waiting for transfers between devices: 64.9 us -> 64.1 us
  transfers between devices with their start and end apart: 20 -> 28, of which waited for: 18 -> 20; matrix products, arithmetic and copies ran while one was open for 17% -> 23% of each run, Pallas kernels for 0% -> 0%
where the time goes in v1:
time: 846 us; the launch traced here: 835 us
  waiting for transfers between devices  514 us (61%)
  matrix products  94.7 us (11%)
  blocking collectives  73.4 us (9%)
  other arithmetic  70.8 us (8%)
  local copies, waits for them, and re-layouts  58 us (7%)
  between operations  15.6 us (2%)
  starting transfers between devices  8.82 us (1%)
    reduce_scatter x3, waiting for transfers between devices, reduce_rows(): lax.psum_scatter(term.astype(BF16), 'shard', scatter_dimension=0, tiled=T...  146 us
    reduce_scatter x4, waiting for transfers between devices, scatter_rep(): lax.psum_scatter(a.astype(BF16), 'rep', scatter_dimension=0, tiled=True)  77.9 us
    reduce_scatter x1, waiting for transfers between devices, per_device(): g_out = lax.psum_scatter(out_term, 'shard', scatter_dimension=0, tiled=True)  72.3 us
    dot_general x12, matrix products, dot(): lax.dot_general(a, b, (((ca,), (cb,)), ((), ())), preferred_element_type=...  69.2 us
    unnamed x17, waiting for transfers between devices  64.1 us
    ppermute x8, waiting for transfers between devices, ring_gather(): earlier.append(lax.ppermute(earlier[-1], axis, up))  56.9 us
    all_gather x1, waiting for transfers between devices, per_device(): wd = lax.all_gather(mine_down, 'shard', axis=0, tiled=True)  48.6 us
    concatenate x4, other arithmetic, ring_gather(): jnp.roll(line, (lax.axis_index(axis) - ways // 2) * shard.shape[dim], axi...  42.5 us
  transfers between devices with their start and end apart: 28, of which 20 were waited for; matrix products, arithmetic and copies ran while one was open for 23% of the time, Pallas kernels for 0%

profile of v1, /device:TPU:0, one launch (start us, length us, event | category | flops | bytes accessed | tf_op | source)
XLA Modules:
  0.0 834.8 jit_solution(12555434138884190740)
XLA Ops:
  10.3 32.7 %all-gather.3 = bf16[8,144,8]{1,2,0:T(8,128)(2,1)S(1)} all-gather(bf16[1,144,8]{1,2,0:T(8,128)(2,1)} %bitcast.153), channel_id=1, replica_groups=mesh['rep'=4,'shard'=8] {'shard'}, dimensions={0}, use_global_device_ids=true | all-gather | bytes 20736 | tf_op jit(solution)/shard_map/all_gather | solution.py:85
  46.9 12.1 %collective-permute-done = bf16[256,1152]{1,0:T(8,128)(2,1)S(1)} collective-permute-done((bf16[256,1152]{1,0:T(8,128)(2,1)S(1)}, bf16[256,1152]{1,0:T(8,128)(2,1)S(1)}, u32[]{:S(2)}, u32[]{:S(2)}) %collective-permute-start) | collective-permute-done | bytes 589856 | tf_op jit(solution)/shard_map/ppermute | solution.py:21
  59.7 8.6 %collective-permute-done.1 = bf16[256,1152]{1,0:T(8,128)(2,1)} collective-permute-done((bf16[256,1152]{1,0:T(8,128)(2,1)S(1)}, bf16[256,1152]{1,0:T(8,128)(2,1)}, u32[]{:S(2)}, u32[]{:S(2)}) %collective-permute-start.1) | collective-permute-done | bytes 589856 | tf_op jit(solution)/shard_map/ppermute | solution.py:21
  68.4 10.1 %fusion.44 = bf16[1024,1152]{1,0:T(8,128)(2,1)} fusion(s32[]{:T(128)S(6)} %select_n.44, bf16[256,1152]{1,0:T(8,128)(2,1)} %collective-permute-done.1, bf16[256,1152]{1,0:T(8,128)(2,1)S(1)} %collective-permute-done, bf16[256,1152]{1,0:T(8,128)(2,1)S(1)} %fusion.71, bf16[256,1152]{1,0:T(8,128)(2,1)} %collective-permute-done.2), kind=kLoop, calls=%fused_computation.87 | loop fusion | flops 18874368 | bytes 4718596 | tf_op jit(solution)/shard_map/jit(_roll_dynamic)/concatenate | solution.py:25
  95.9 22.1 %all-gather.13.cloned.1.call-done = bf16[1152,1152]{1,0:T(8,128)(2,1)} async-done(((bf16[144,1152]{1,0:T(8,128)(2,1)}), bf16[1152,1152]{1,0:T(8,128)(2,1)}) %all-gather.13.cloned.1.call-update) | async-done | bytes 2654224 | tf_op jit(solution)/shard_map/all_gather | solution.py:82
  125.5 28.1 %reduce-scatter.12.cloned.1.call-done = bf16[256,1152]{1,0:T(8,128)(2,1)} async-done(((bf16[1024,1152]{1,0:T(8,128)(2,1)}), bf16[256,1152]{1,0:T(8,128)(2,1)}) %reduce-scatter.12.cloned.1.call-update) | async-done | bytes 589840 | tf_op jit(solution)/shard_map/reduce_scatter | solution.py:62
  161.2 10.7 %collective-permute-done.3 = bf16[256,1152]{1,0:T(8,128)(2,1)S(1)} collective-permute-done((bf16[256,1152]{1,0:T(8,128)(2,1)S(1)}, bf16[256,1152]{1,0:T(8,128)(2,1)S(1)}, u32[]{:S(2)}, u32[]{:S(2)}) %collective-permute-start.3) | collective-permute-done | bytes 589856 | tf_op jit(solution)/shard_map/ppermute | solution.py:21
  172.4 12.2 %collective-permute-done.7 = bf16[256,1152]{1,0:T(8,128)(2,1)S(1)} collective-permute-done((bf16[256,1152]{1,0:T(8,128)(2,1)S(1)}, bf16[256,1152]{1,0:T(8,128)(2,1)S(1)}, u32[]{:S(2)}, u32[]{:S(2)}) %collective-permute-start.7) | collective-permute-done | bytes 589856 | tf_op jit(solution)/shard_map/ppermute | solution.py:21
  184.5 11.4 %fusion.30 = bf16[1024,1152]{1,0:T(8,128)(2,1)} fusion(s32[]{:T(128)S(6)} %select_n.44, bf16[256,1152]{1,0:T(8,128)(2,1)S(1)} %collective-permute-done.7, bf16[256,1152]{1,0:T(8,128)(2,1)S(1)} %collective-permute-done.6, bf16[256,1152]{1,0:T(8,128)(2,1)S(1)} %bitcast.147, bf16[256,1152]{1,0:T(8,128)(2,1)S(1)} %collective-permute-done.8), kind=kLoop, calls=%fused_computation.73 | loop fusion | flops 18874368 | bytes 4718596 | tf_op jit(solution)/shard_map/jit(_roll_dynamic)/concatenate | solution.py:25
  196.0 11.5 %fusion.37 = bf16[1024,1152]{1,0:T(8,128)(2,1)} fusion(s32[]{:T(128)S(6)} %select_n.44, bf16[256,1152]{1,0:T(8,128)(2,1)S(1)} %collective-permute-done.4, bf16[256,1152]{1,0:T(8,128)(2,1)S(1)} %collective-permute-done.3, bf16[256,1152]{1,0:T(8,128)(2,1)S(1)} %add_convert_fusion.1, bf16[256,1152]{1,0:T(8,128)(2,1)S(1)} %collective-permute-done.5), kind=kLoop, calls=%fused_computation.80 | loop fusion | flops 18874368 | bytes 4718596 | tf_op jit(solution)/shard_map/jit(_roll_dynamic)/concatenate | solution.py:25
  211.2 7.5 convolution_add_fusion
  218.8 48.6 %all-gather.17.cloned.1.call-done = bf16[1152,1076]{1,0:T(8,128)(2,1)} async-done(((bf16[144,1076]{1,0:T(8,128)(2,1)}), bf16[1152,1076]{1,0:T(8,128)(2,1)}) %all-gather.17.cloned.1.call-update) | async-done | bytes 2479120 | tf_op jit(solution)/shard_map/all_gather | solution.py:84
  267.4 9.1 %fusion.120 = (f32[1076]{0:T(1024)S(1)}, bf16[1024,1076]{0,1:T(8,128)(2,1)S(1)}) fusion(f32[1024,1076]{0,1:T(8,128)} %convolution_add_fusion, bf16[1024,1152]{1,0:T(8,128)(2,1)} %fusion.30, bf16[1152,1076]{1,0:T(8,128)(2,1)} %all-gather.17.cloned.1.call-done), kind=kOutput, calls=%fused_computation.207 | convolution fusion | flops 2560637952 | bytes 11453648 | tf_op jit(solution)/shard_map/dot_general | solution.py:29
  282.9 7.1 convolution_convert_fusion.1
  290.5 8.9 %convolution_convert_fusion.5 = bf16[1024,1152]{1,0:T(8,128)(2,1)} fusion(bf16[1152,1076]{1,0:T(8,128)(2,1)} %all-gather.17.cloned.1.call-done, f32[1024,1076]{0,1:T(8,128)} %convolution_add_fusion), kind=kOutput, calls=%fused_computation.53 | convolution fusion | flops 2549698560 | bytes 9245696 | tf_op jit(solution)/shard_map/dot_general | solution.py:29
  299.4 8.0 convolution_convert_fusion
  316.2 73.7 %reduce-scatter.24.cloned.1.call-done = bf16[144,1076]{1,0:T(8,128)(2,1)} async-done(((bf16[1152,1076]{1,0:T(8,128)(2,1)}), bf16[144,1076]{1,0:T(8,128)(2,1)}) %reduce-scatter.24.cloned.1.call-update) | async-done | bytes 309904 | tf_op jit(solution)/shard_map/reduce_scatter | solution.py:121
  390.0 34.8 %reduce-scatter.14.cloned.1.call-done = bf16[256,1152]{1,0:T(8,128)(2,1)} async-done(((bf16[1024,1152]{1,0:T(8,128)(2,1)}), bf16[256,1152]{1,0:T(8,128)(2,1)}) %reduce-scatter.14.cloned.1.call-update) | async-done | bytes 589840 | tf_op jit(solution)/shard_map/reduce_scatter | solution.py:62
  429.6 13.2 %collective-permute-done.9 = bf16[256,1152]{1,0:T(8,128)(2,1)S(1)} collective-permute-done((bf16[256,1152]{1,0:T(8,128)(2,1)S(1)}, bf16[256,1152]{1,0:T(8,128)(2,1)S(1)}, u32[]{:S(2)}, u32[]{:S(2)}) %collective-permute-start.9) | collective-permute-done | bytes 589856 | tf_op jit(solution)/shard_map/ppermute | solution.py:21
  442.8 57.2 %reduce-scatter.26.cloned.1.call-done = bf16[144,1076]{1,0:T(8,128)(2,1)} async-done(((bf16[1152,1076]{1,0:T(8,128)(2,1)}), bf16[144,1076]{1,0:T(8,128)(2,1)}) %reduce-scatter.26.cloned.1.call-update) | async-done | bytes 309904 | tf_op jit(solution)/shard_map/reduce_scatter | solution.py:121
  500.1 9.3 %fusion.23 = bf16[1024,1152]{1,0:T(8,128)(2,1)S(1)} fusion(s32[]{:T(128)S(6)} %select_n.44, bf16[256,1152]{1,0:T(8,128)(2,1)} %collective-permute-done.10, bf16[256,1152]{1,0:T(8,128)(2,1)S(1)} %collective-permute-done.9, bf16[256,1152]{1,0:T(8,128)(2,1)S(1)} %convert_element_type.137, bf16[256,1152]{1,0:T(8,128)(2,1)} %collective-permute-done.11), kind=kLoop, calls=%fused_computation.66 | loop fusion | flops 18874368 | bytes 4718596 | tf_op jit(solution)/shard_map/jit(_roll_dynamic)/concatenate | solution.py:25
  521.2 8.6 %fusion.66 = f32[4,256,4,72]{1,3,2,0:T(8,128)} fusion(f32[4,4,256,256]{2,3,1,0:T(8,128)} %fusion.97, bf16[4,256,4,72]{1,0,3,2:T(4,128)(2,1)} %reshape.133, f32[4,4,256,256]{2,3,1,0:T(8,128)} %copy-done.6, f32[4,4,256]{2,1,0:T(4,128)S(1)} %get-tuple-element.44), kind=kOutput, calls=%fused_computation.119 | convolution fusion | flops 158339328 | bytes 10174464 | tf_op jit(solution)/shard_map/bhqk,bqhd->bkhd/dot_general | solution.py:33
  533.1 8.5 %fusion.63 = f32[4,256,4,72]{1,3,2,0:T(8,128)} fusion(f32[4,4,256,256]{2,3,1,0:T(8,128)} %fusion.97, bf16[4,256,4,72]{1,0,3,2:T(4,128)(2,1)} %copy-done.12, f32[4,4,256,256]{2,3,1,0:T(8,128)} %copy-done.6, f32[4,4,256]{2,1,0:T(4,128)S(1)} %get-tuple-element.44), kind=kOutput, calls=%fused_computation.118 | convolution fusion | flops 158339328 | bytes 10174464 | tf_op jit(solution)/shard_map/bhqk,bkhd->bqhd/dot_general | solution.py:33
  551.1 7.0 convolution_convert_fusion.2
  564.6 19.5 %psum.23 = f32[1076]{0:T(1024)S(1)} all-reduce(f32[1076]{0:T(1024)S(1)} %get-tuple-element.46), channel_id=1, replica_groups=mesh['rep'=4,'shard'=8] {'shard'}, use_global_device_ids=true, to_apply=%region_30.32 | all-reduce | flops 1076 | bytes 8608 | tf_op jit(solution)/shard_map/psum | solution.py:170
  603.2 14.6 %reduce-scatter.20.cloned.1.call-done = bf16[144,864]{1,0:T(8,128)(2,1)} async-done(((bf16[1152,864]{1,0:T(8,128)(2,1)}), bf16[144,864]{1,0:T(8,128)(2,1)}) %reduce-scatter.20.cloned.1.call-update) | async-done | bytes 248848 | tf_op jit(solution)/shard_map/reduce_scatter | solution.py:121
  617.8 10.4 %all-gather = bf16[576,864]{1,0:T(8,128)(2,1)S(1)} all-gather(bf16[144,864]{1,0:T(8,128)(2,1)} %reduce-scatter.20.cloned.1.call-done), channel_id=2, replica_groups=mesh['rep'=4,'shard'=8] {'rep'}, dimensions={0}, use_global_device_ids=true | all-gather | bytes 1244160 | tf_op jit(solution)/shard_map/all_gather | solution.py:173
  644.1 8.1 reduce-scatter.18.cloned.1.call-done
  655.1 72.3 %reduce-scatter.22.cloned.1.call-done = bf16[144,1152]{1,0:T(8,128)(2,1)} async-done(((bf16[1152,1152]{1,0:T(8,128)(2,1)}), bf16[144,1152]{1,0:T(8,128)(2,1)}) %reduce-scatter.22.cloned.1.call-update) | async-done | bytes 331792 | tf_op jit(solution)/shard_map/reduce_scatter | solution.py:137
  729.8 63.1 %reduce-scatter.28.cloned.1.call-done = f32[144,8]{1,0:T(8,128)} async-done(((f32[1152,8]{1,0:T(8,128)}), f32[144,8]{1,0:T(8,128)}) %reduce-scatter.28.cloned.1.call-update) | async-done | bytes 4624
  793.9 10.9 %all-reduce.1 = (f32[144,8]{0,1:T(8,128)}, f32[4304]{0:T(1024)}) all-reduce(f32[144,8]{0,1:T(8,128)S(1)} %copy.95, f32[4304]{0:T(1024)S(1)} %dynamic-update-slice), channel_id=1, replica_groups=mesh['rep'=4,'shard'=8] {'rep'}, use_global_device_ids=true, to_apply=%region_28.30 | all-reduce | flops 5456 | bytes 43648 | tf_op jit(solution)/shard_map/psum | solution.py:169
  804.7 21.2 %all-reduce.4.cloned.1.call-done = bf16[144,1152]{1,0:T(8,128)(2,1)} async-done(((bf16[144,1152]{1,0:T(8,128)(2,1)}), bf16[144,1152]{1,0:T(8,128)(2,1)}) %all-reduce.4.cloned.1.call-update) | async-done | bytes 331792 | tf_op jit(solution)/shard_map/psum | solution.py:178
  (188 shorter events, 137.9 us)
Async XLA Ops:
  7.2 115.3 %copy-start = (bf16[144,4304]{1,0:T(8,128)(2,1)S(1)}, bf16[144,4304]{1,0:T(8,128)(2,1)}, u32[]{:S(2)}) copy-start(bf16[144,4304]{1,0:T(8,128)(2,1)} %param.14) | copy-start | bytes 3718660
  7.2 37.2 %copy-start.2 = (bf16[1,256,1152]{2,1,0:T(8,128)(2,1)S(1)}, bf16[1,256,1152]{2,1,0:T(8,128)(2,1)}, u32[]{:S(2)}) copy-start(bf16[1,256,1152]{2,1,0:T(8,128)(2,1)} %param.10) | copy-start | bytes 1769476
  7.2 71.3 %all-gather.11.cloned.1.call-start = ((), (), s32[]{:S(2)}) async-start(), calls=%async_computation.9 | async-start | bytes 2322432 | tf_op jit(solution)/shard_map/all_gather | solution.py:81
  9.5 108.5 %all-gather.13.cloned.1.call-start = ((), (), s32[]{:S(2)}) async-start(), calls=%async_computation.10 | async-start | bytes 2985984 | tf_op jit(solution)/shard_map/all_gather | solution.py:82
  10.2 143.4 %reduce-scatter.12.cloned.1.call-start = ((), (), s32[]{:S(2)}) async-start(), calls=%async_computation.11 | async-start | bytes 2949120 | tf_op jit(solution)/shard_map/reduce_scatter | solution.py:62
  45.1 13.9 %collective-permute-start = (bf16[256,1152]{1,0:T(8,128)(2,1)S(1)}, bf16[256,1152]{1,0:T(8,128)(2,1)S(1)}, u32[]{:S(2)}, u32[]{:S(2)}) collective-permute-start(bf16[256,1152]{1,0:T(8,128)(2,1)S(1)} %fusion.71), channel_id=1, source_target_pairs={{0,8},{8,16},{16,24},{24,0},{1,9},{9,17},{17,25},{25,1},{2,10},{10... | collective-permute-start | bytes 1769480 | tf_op jit(solution)/shard_map/ppermute | solution.py:21
  45.1 14.6 %collective-permute-start.2 = (bf16[256,1152]{1,0:T(8,128)(2,1)S(1)}, bf16[256,1152]{1,0:T(8,128)(2,1)}, u32[]{:S(2)}, u32[]{:S(2)}) collective-permute-start(bf16[256,1152]{1,0:T(8,128)(2,1)S(1)} %fusion.71), channel_id=1, source_target_pairs={{0,24},{8,0},{16,8},{24,16},{1,25},{9,1},{17,9},{25,17},{2,26},{10... | collective-permute-start | bytes 1769480 | tf_op jit(solution)/shard_map/ppermute | solution.py:23
  59.0 9.4 %collective-permute-start.1 = (bf16[256,1152]{1,0:T(8,128)(2,1)S(1)}, bf16[256,1152]{1,0:T(8,128)(2,1)}, u32[]{:S(2)}, u32[]{:S(2)}) collective-permute-start(bf16[256,1152]{1,0:T(8,128)(2,1)S(1)} %collective-permute-done), channel_id=1, source_target_pairs={{0,8},{8,16},{16,24},{24,0},{1,9},{9,17},{17,25},{25,1},{2,10},{10... | collective-permute-start | bytes 1769480 | tf_op jit(solution)/shard_map/ppermute | solution.py:21
  122.1 89.2 %all-gather.15.cloned.1.call-start = ((), (), s32[]{:S(2)}) async-start(), calls=%async_computation.12 | async-start | bytes 2985984 | tf_op jit(solution)/shard_map/all_gather | solution.py:83
  123.4 144.0 %all-gather.17.cloned.1.call-start = ((), (), s32[]{:S(2)}) async-start(), calls=%async_computation.13 | async-start | bytes 2985984 | tf_op jit(solution)/shard_map/all_gather | solution.py:84
  123.4 35.2 %collective-permute-start.6 = (bf16[256,1152]{1,0:T(8,128)(2,1)S(1)}, bf16[256,1152]{1,0:T(8,128)(2,1)S(1)}, u32[]{:S(2)}, u32[]{:S(2)}) collective-permute-start(bf16[256,1152]{1,0:T(8,128)(2,1)S(1)} %bitcast.145), channel_id=1, source_target_pairs={{0,8},{8,16},{16,24},{24,0},{1,9},{9,17},{17,25},{25,1},{2,10},{10... | collective-permute-start | bytes 1769480 | tf_op jit(solution)/shard_map/ppermute | solution.py:21
  125.4 189.0 %reduce-scatter.16.cloned.1.call-start = ((), (), s32[]{:S(2)}) async-start(), calls=%async_computation.15 | async-start | bytes 2949120 | tf_op jit(solution)/shard_map/reduce_scatter | solution.py:62
  156.8 15.0 %collective-permute-start.3 = (bf16[256,1152]{1,0:T(8,128)(2,1)S(1)}, bf16[256,1152]{1,0:T(8,128)(2,1)S(1)}, u32[]{:S(2)}, u32[]{:S(2)}) collective-permute-start(bf16[256,1152]{1,0:T(8,128)(2,1)S(1)} %add_convert_fusion.1), channel_id=1, source_target_pairs={{0,8},{8,16},{16,24},{24,0},{1,9},{9,17},{17,25},{25,1},{2,10},{10... | collective-permute-start | bytes 1769480 | tf_op jit(solution)/shard_map/ppermute | solution.py:21
  156.9 15.5 %collective-permute-start.8 = (bf16[256,1152]{1,0:T(8,128)(2,1)S(1)}, bf16[256,1152]{1,0:T(8,128)(2,1)S(1)}, u32[]{:S(2)}, u32[]{:S(2)}) collective-permute-start(bf16[256,1152]{1,0:T(8,128)(2,1)S(1)} %bitcast.146), channel_id=1, source_target_pairs={{0,24},{8,0},{16,8},{24,16},{1,25},{9,1},{17,9},{25,17},{2,26},{10... | collective-permute-start | bytes 1769480 | tf_op jit(solution)/shard_map/ppermute | solution.py:23
  158.6 25.9 %collective-permute-start.7 = (bf16[256,1152]{1,0:T(8,128)(2,1)S(1)}, bf16[256,1152]{1,0:T(8,128)(2,1)S(1)}, u32[]{:S(2)}, u32[]{:S(2)}) collective-permute-start(bf16[256,1152]{1,0:T(8,128)(2,1)S(1)} %collective-permute-done.6), channel_id=1, source_target_pairs={{0,8},{8,16},{16,24},{24,0},{1,9},{9,17},{17,25},{25,1},{2,10},{10... | collective-permute-start | bytes 1769480 | tf_op jit(solution)/shard_map/ppermute | solution.py:21
  159.4 36.5 %collective-permute-start.5 = (bf16[256,1152]{1,0:T(8,128)(2,1)S(1)}, bf16[256,1152]{1,0:T(8,128)(2,1)S(1)}, u32[]{:S(2)}, u32[]{:S(2)}) collective-permute-start(bf16[256,1152]{1,0:T(8,128)(2,1)S(1)} %add_convert_fusion.1), channel_id=1, source_target_pairs={{0,24},{8,0},{16,8},{24,16},{1,25},{9,1},{17,9},{25,17},{2,26},{10... | collective-permute-start | bytes 1769480 | tf_op jit(solution)/shard_map/ppermute | solution.py:23
  171.9 24.1 %collective-permute-start.4 = (bf16[256,1152]{1,0:T(8,128)(2,1)S(1)}, bf16[256,1152]{1,0:T(8,128)(2,1)S(1)}, u32[]{:S(2)}, u32[]{:S(2)}) collective-permute-start(bf16[256,1152]{1,0:T(8,128)(2,1)S(1)} %collective-permute-done.3), channel_id=1, source_target_pairs={{0,8},{8,16},{16,24},{24,0},{1,9},{9,17},{17,25},{25,1},{2,10},{10... | collective-permute-start | bytes 1769480 | tf_op jit(solution)/shard_map/ppermute | solution.py:21
  282.9 107.0 %reduce-scatter.24.cloned.1.call-start = ((), (), s32[]{:S(2)}) async-start(), calls=%async_computation.20 | async-start | bytes 2985984 | tf_op jit(solution)/shard_map/reduce_scatter | solution.py:121
  290.0 134.8 %reduce-scatter.14.cloned.1.call-start = ((), (), s32[]{:S(2)}) async-start(), calls=%async_computation.14 | async-start | bytes 2949120 | tf_op jit(solution)/shard_map/reduce_scatter | solution.py:62
  299.4 200.7 %reduce-scatter.26.cloned.1.call-start = ((), (), s32[]{:S(2)}) async-start(), calls=%async_computation.21 | async-start | bytes 2985984 | tf_op jit(solution)/shard_map/reduce_scatter | solution.py:121
  307.4 117.4 %copy-start.8 = (bf16[1,256,1152]{2,1,0:T(8,128)(2,1)S(1)}, bf16[1,256,1152]{2,1,0:T(8,128)(2,1)}, u32[]{:S(2)}) copy-start(bf16[1,256,1152]{2,1,0:T(8,128)(2,1)} %param.11) | copy-start | bytes 1769476
  307.4 279.8 %all-gather.19.cloned.1.call-start = ((), (), s32[]{:S(2)}) async-start(), calls=%async_computation.22 | async-start | bytes 1658880 | tf_op jit(solution)/shard_map/all_gather | solution.py:173
  389.9 205.3 %all-gather.21.cloned.1.call-start = ((), (), s32[]{:S(2)}) async-start(), calls=%async_computation.23 | async-start | bytes 1658880 | tf_op jit(solution)/shard_map/all_gather | solution.py:173
  427.8 15.0 %collective-permute-start.9 = (bf16[256,1152]{1,0:T(8,128)(2,1)S(1)}, bf16[256,1152]{1,0:T(8,128)(2,1)S(1)}, u32[]{:S(2)}, u32[]{:S(2)}) collective-permute-start(bf16[256,1152]{1,0:T(8,128)(2,1)S(1)} %convert_element_type.137), channel_id=1, source_target_pairs={{0,8},{8,16},{16,24},{24,0},{1,9},{9,17},{17,25},{25,1},{2,10},{10... | collective-permute-start | bytes 1769480 | tf_op jit(solution)/shard_map/ppermute | solution.py:21
  427.9 72.3 %collective-permute-start.11 = (bf16[256,1152]{1,0:T(8,128)(2,1)S(1)}, bf16[256,1152]{1,0:T(8,128)(2,1)}, u32[]{:S(2)}, u32[]{:S(2)}) collective-permute-start(bf16[256,1152]{1,0:T(8,128)(2,1)S(1)} %convert_element_type.137), channel_id=1, source_target_pairs={{0,24},{8,0},{16,8},{24,16},{1,25},{9,1},{17,9},{25,17},{2,26},{10... | collective-permute-start | bytes 1769480 | tf_op jit(solution)/shard_map/ppermute | solution.py:23
  442.8 57.3 %collective-permute-start.10 = (bf16[256,1152]{1,0:T(8,128)(2,1)S(1)}, bf16[256,1152]{1,0:T(8,128)(2,1)}, u32[]{:S(2)}, u32[]{:S(2)}) collective-permute-start(bf16[256,1152]{1,0:T(8,128)(2,1)S(1)} %collective-permute-done.9), channel_id=1, source_target_pairs={{0,8},{8,16},{16,24},{24,0},{1,9},{9,17},{17,25},{25,1},{2,10},{10... | collective-permute-start | bytes 1769480 | tf_op jit(solution)/shard_map/ppermute | solution.py:21
  500.1 117.8 %reduce-scatter.20.cloned.1.call-start = ((), (), s32[]{:S(2)}) async-start(), calls=%async_computation.17 | async-start | bytes 2322432 | tf_op jit(solution)/shard_map/reduce_scatter | solution.py:121
  550.8 101.4 %reduce-scatter.18.cloned.1.call-start = ((), (), s32[]{:S(2)}) async-start(), calls=%async_computation.16 | async-start | bytes 2949120 | tf_op jit(solution)/shard_map/reduce_scatter | solution.py:62
  558.1 169.3 %reduce-scatter.22.cloned.1.call-start = ((), (), s32[]{:S(2)}) async-start(), calls=%async_computation.18 | async-start | bytes 2985984 | tf_op jit(solution)/shard_map/reduce_scatter | solution.py:137
  562.7 230.2 %reduce-scatter.28.cloned.1.call-start = ((), (), s32[]{:S(2)}) async-start(), calls=%async_computation.24 | async-start | bytes 663552
  653.9 173.9 %copy-start.1 = (bf16[144,4304]{1,0:T(8,128)(2,1)S(1)}, bf16[144,4304]{1,0:T(8,128)(2,1)}, u32[]{:S(2)}) copy-start(bf16[144,4304]{1,0:T(8,128)(2,1)} %param.14) | copy-start | bytes 3718660
  655.0 170.9 %all-reduce.4.cloned.1.call-start = ((), (), s32[]{:S(2)}) async-start(), calls=%async_computation.19 | async-start | bytes 663552 | tf_op jit(solution)/shard_map/psum | solution.py:178
  (18 other events, 67.5 us)
Sparse Core Ops, SparseCore 0:
  10.8 51.4 all-gather.10
  64.4 53.5 all-gather.12
  122.2 31.3 reduce-scatter.11
  156.2 54.9 all-gather.14
  213.8 53.5 all-gather.16
  283.0 31.4 reduce-scatter.15
  318.1 71.7 reduce-scatter.23
  393.0 31.7 reduce-scatter.13
  428.5 71.5 reduce-scatter.25
  501.4 17.2 all-gather.18
  520.3 18.2 all-gather.20
  550.9 66.8 reduce-scatter.19
  620.3 31.7 reduce-scatter.17
  655.7 71.6 reduce-scatter.21
  731.1 61.7 reduce-scatter.27
  795.1 30.7 all-reduce.3
